TPU v7x, 32 devices: a whole 2x2x4 slice. The times are simulated.
32 devices in a mesh: dev: 16 (over z, y, x), rep: 2 (over core).
Axes of the slice: x: 2, y: 2, z: 4, core: 2. Of those that a mesh axis runs over, the one named last changes fastest.
Arguments:
- tables: bfloat16 [64, 2048, 128], P('dev'), may hold values from -1.5 to 1.5
- bag_rows: int32 [32, 64, 32, 4], P(('rep', 'dev')), parts along dimension 0, may hold values from 0 to 2047
- bag_lengths: int32 [32, 64, 32], P(('rep', 'dev')), parts along dimension 0, may hold values from 1 to 4
- row_counts: int32 [32, 64], P(('rep', 'dev')), parts along dimension 0, may hold values from 1 to 32, as said below
- inverse: int32 [4096, 64], P(('rep', 'dev')), parts along dimension 0, may hold values from 0 to 31
- table_order: int32 [64], replicated, may hold values from 0 to 63, each once
- compress: bfloat16 [16, 64], replicated, may hold values from -0.75 to 0.75
- top_weight: bfloat16 [1024, 512], replicated, may hold values from -0.1875 to 0.1875
- top_bias: float32 [512], replicated, may hold values from -1.8 to 1.8
Outputs:
- ranked: bfloat16 [4096, 512], P(('rep', 'dev')), parts along dimension 0
There are 2 independent parts, one for each index of `rep`. A program takes and returns all parts, laid end to end along the dimension named above; an argument that names none is the same for every part. Nothing has to cross between parts.
Inputs may be any that keep to these rules, and one draw needn't show every extreme that they name: `row_counts`: for every sample device and every aligned group of 4 consecutive slots the counts sum to at most 80; a count of 32 and a group sum of 80 occur in every draw.
All inputs are finite; a program needn't handle non-finite values.
Results may differ from a plain program's by a relative error of at most 0.0062.
Values may be sent and summed in bfloat16 or wider, within the bound.
A program may use at most 128 MiB of HBM per device.

v0:
```python
import functools

import jax
import jax.numpy as jnp
from jax import lax
from jax.experimental import pallas as pl
from jax.experimental.pallas import tpu as pltpu
from jax.sharding import PartitionSpec as P

F32 = jnp.float32
BF16 = jnp.bfloat16


def select_samples(
    most, inv_ref, order_ref, counts_ref, compress_ref, sel, spread_c, mask
):
    features, samples = inv_ref.shape
    per = 8
    span = per * most
    inv = inv_ref[...].astype(F32).T.astype(BF16)
    comp = compress_ref[...]

    def select(c, carry):
        lane = lax.broadcasted_iota(jnp.int32, (1, span), 1)
        slot, unit = lane // most, lane % most
        order_row = jnp.zeros((1, span), jnp.int32)
        count_row = jnp.zeros((1, span), jnp.int32)
        row_u = lax.broadcasted_iota(jnp.int32, (most, samples), 0)
        for i in range(per):
            s = c * per + i
            f, count = order_ref[s], counts_ref[s]
            order_row = jnp.where(slot == i, f, order_row)
            count_row = jnp.where(slot == i, count, count_row)
            wanted = inv_ref[pl.ds(f, 1), :]
            hit = jnp.logical_and(row_u == wanted, row_u < count)
            mask[pl.ds(pl.multiple_of(s * most, most), most), :] = jnp.where(hit, 1.0, 0.0)
        target = jnp.where(unit < count_row, unit, -1).astype(F32)
        feature = lax.broadcasted_iota(jnp.int32, (features, span), 0)
        one_hot = jnp.where(feature == order_row, 1.0, 0.0).astype(BF16)
        inv_all = jnp.dot(inv, one_hot, preferred_element_type=F32)
        columns = pl.ds(pl.multiple_of(c * span, span), span)
        sel[:, columns] = jnp.where(inv_all == target, 1.0, 0.0).astype(BF16)
        spread_c[:, columns] = jnp.dot(comp, one_hot, preferred_element_type=F32)
        return carry

    lax.fori_loop(0, features // per, select, 0)


def exchange_kernel(
    n, most, bags_ref, tables_ref, inv_ref, order_ref, counts_ref, compress_ref,
    rows_ref, sel, spread_c, mask,
    tab16, tab32, ids_out, ids_in, pooled, staging,
    tab_sem, id_send, id_recv, smem_sem, row_send, row_recv,
):
    me = lax.axis_index("dev")
    tabs, vocab, width = tables_ref.shape
    spread = bags_ref.shape[0]
    pooling = spread // most
    zero_row = tabs * vocab

    table_copy = pltpu.make_async_copy(tables_ref, tab16, tab_sem)
    table_copy.start()
    barrier = pltpu.get_barrier_semaphore()

    def greet(i, carry):
        pl.semaphore_signal(barrier, inc=1, device_id={"dev": lax.rem(me + i, n)})
        return carry

    lax.fori_loop(1, n, greet, 0)

    index = bags_ref[...].T
    for g in range(n):
        ids_out[g] = index[g * tabs:(g + 1) * tabs]

    pl.semaphore_wait(barrier, n - 1)

    def id_copy(i):
        peer = lax.rem(me + i, n)
        return pltpu.make_async_remote_copy(
            src_ref=ids_out.at[peer], dst_ref=ids_in.at[me],
            send_sem=id_send.at[peer], recv_sem=id_recv.at[me],
            device_id={"dev": peer},
        )

    def id_arrival(source):
        return pltpu.make_async_remote_copy(
            src_ref=ids_out.at[source], dst_ref=ids_in.at[source],
            send_sem=id_send.at[source], recv_sem=id_recv.at[source],
            device_id={"dev": source},
        )

    def offset(j):
        half = (j + 1) // 2
        return n // 2 + jnp.where(j % 2 == 1, half, -half)

    def send_ids(j, carry):
        id_copy(offset(j)).start()
        return carry

    lax.fori_loop(0, n - 1, send_ids, 0)

    own_ids = pltpu.make_async_copy(ids_out.at[me], ids_in.at[me], smem_sem)
    own_ids.start()
    table_copy.wait()
    tab32[pl.ds(zero_row, 8), :] = jnp.zeros((8, width), F32)
    step = 256

    def widen(i, carry):
        for t in range(tabs):
            base = pl.multiple_of(i * step, step)
            tab32[pl.ds(t * vocab + base, step), :] = tab16[t, pl.ds(base, step), :].astype(F32)
        return carry

    lax.fori_loop(0, vocab // step, widen, 0)

    def pool(source, store):
        def one_table(t, carry):
            at_table = pl.multiple_of(t * most, most)
            for r in range(most):
                total = None
                for p in range(pooling):
                    row = tab32[pl.ds(ids_in[source, t, r * pooling + p], 1), :]
                    total = row if total is None else total + row
                pooled[pl.ds(at_table + r, 1), :] = total
            return carry

        lax.fori_loop(0, tabs, one_table, 0)
        store(pooled[...].astype(BF16))

    def row_copy(peer):
        return pltpu.make_async_remote_copy(
            src_ref=staging.at[peer], dst_ref=rows_ref.at[me],
            send_sem=row_send.at[peer], recv_sem=row_recv.at[me],
            device_id={"dev": peer},
        )

    def serve(j, carry):
        peer = lax.rem(me + offset(j), n)
        id_arrival(peer).wait_recv()

        def store(value):
            staging[peer] = value

        pool(peer, store)
        row_copy(peer).start()
        return carry

    lax.fori_loop(0, n - 1, serve, 0)

    own_ids.wait()

    def store_own(value):
        rows_ref[me] = value

    pool(me, store_own)
    select_samples(most, inv_ref, order_ref, counts_ref, compress_ref, sel, spread_c, mask)

    def finish(i, carry):
        peer = lax.rem(me + i, n)
        id_copy(i).wait_send()
        row_copy(peer).wait_send()
        pltpu.make_async_remote_copy(
            src_ref=staging.at[peer], dst_ref=rows_ref.at[peer],
            send_sem=row_send.at[peer], recv_sem=row_recv.at[peer],
            device_id={"dev": peer},
        ).wait_recv()
        return carry

    lax.fori_loop(1, n, finish, 0)


def exchange(n, most, bags, tables, inv, order, counts, compress):
    tabs, vocab, width = tables.shape
    spread, slots = bags.shape
    block = tabs * most
    total, samples, mixes = n * block, inv.shape[1], compress.shape[0]
    vmem = pl.BlockSpec(memory_space=pltpu.VMEM)
    smem = pl.BlockSpec(memory_space=pltpu.SMEM)
    return pl.pallas_call(
        functools.partial(exchange_kernel, n, most),
        out_shape=[
            jax.ShapeDtypeStruct((n, block, width), BF16),
            jax.ShapeDtypeStruct((samples, total), BF16),
            jax.ShapeDtypeStruct((mixes, total), F32),
            jax.ShapeDtypeStruct((total, samples), F32),
        ],
        in_specs=[vmem, pl.BlockSpec(memory_space=pl.ANY), vmem, smem, smem, vmem],
        out_specs=[vmem] * 4,
        scratch_shapes=[
            pltpu.VMEM(tables.shape, BF16),
            pltpu.VMEM((tabs * vocab + 8, width), F32),
            pltpu.VMEM((n, tabs, spread), jnp.int32),
            pltpu.SMEM((n, tabs, spread), jnp.int32),
            pltpu.VMEM((block, width), F32),
            pltpu.VMEM((n, block, width), BF16),
            pltpu.SemaphoreType.DMA,
            pltpu.SemaphoreType.DMA((n,)),
            pltpu.SemaphoreType.DMA((n,)),
            pltpu.SemaphoreType.DMA,
            pltpu.SemaphoreType.DMA((n,)),
            pltpu.SemaphoreType.DMA((n,)),
        ],
        compiler_params=pltpu.CompilerParams(
            collective_id=0, has_side_effects=True, vmem_limit_bytes=50 << 20
        ),
        name="exchange",
    )(bags, tables, inv, order, counts, compress)


def interact_kernel(
    rows_ref, sel, spread_c, mask, order_ref, weight_ref, bias_ref, out_ref, mixed, pairs,
):
    mixes, total = spread_c.shape
    samples = mask.shape[1]
    width = rows_ref.shape[1]
    features = order_ref.shape[0]
    most = total // features
    per = 8
    span = per * most
    deep = min(total, 2048)

    def mix(k, carry):
        acc = jnp.zeros((samples, width), F32)

        def part(q, acc):
            columns = pl.ds(pl.multiple_of(q * deep, deep), deep)
            scaled = sel[:, columns] * spread_c[pl.ds(k, 1), columns].astype(BF16)
            return acc + jnp.dot(scaled, rows_ref[columns, :], preferred_element_type=F32)

        if total == deep:
            acc = part(0, acc)
        else:
            acc = lax.fori_loop(0, total // deep, part, acc)
        mixed[pl.ds(pl.multiple_of(k * samples, samples), samples), :] = acc.astype(BF16)
        return carry

    lax.fori_loop(0, mixes, mix, 0)

    pair = 2

    def inner(j, carry):
        c8, kp = j // (mixes // pair), j % (mixes // pair)
        wanted = mixed[pl.ds(pl.multiple_of(kp * pair * samples, samples), pair * samples), :]
        for i in range(per):
            c = c8 * per + i
            at = pl.ds(pl.multiple_of(c * span, span), span)
            product = lax.dot_general(
                rows_ref[at, :], wanted, (((1,), (1,)), ((), ())), preferred_element_type=F32
            )
            chosen = mask[at, :]
            for h in range(pair):
                kept = product[:, h * samples:(h + 1) * samples] * chosen
                summed = jnp.sum(kept.reshape(per, most, samples), axis=1)
                for s in range(per):
                    f = order_ref[c * per + s]
                    pairs[pl.ds(f * mixes + kp * pair + h, 1), :] = summed[s:s + 1, :]
        return carry

    lax.fori_loop(0, features // (per * per) * (mixes // pair), inner, 0)

    depth = min(features * mixes, 1024)
    hidden = jnp.zeros(out_ref.shape, F32) + bias_ref[...]

    def top(q, hidden):
        at = pl.ds(pl.multiple_of(q * depth, depth), depth)
        return hidden + lax.dot_general(
            pairs[at, :].astype(BF16), weight_ref[at, :], (((0,), (0,)), ((), ())),
            preferred_element_type=F32,
        )

    if depth == features * mixes:
        hidden = top(0, hidden)
    else:
        hidden = lax.fori_loop(0, features * mixes // depth, top, hidden)
    out_ref[...] = jnp.maximum(hidden, 0.0).astype(BF16)


def interact(rows, sel, spread_c, mask, order, weight, bias):
    mixes, total = spread_c.shape
    samples, features, width = mask.shape[1], order.shape[0], rows.shape[1]
    held = rows.size + weight.size + samples * total + 2 * (mixes + samples) * total
    held += mixes * samples * width + 2 * features * mixes * samples
    vmem = pl.BlockSpec(memory_space=pltpu.VMEM)
    smem = pl.BlockSpec(memory_space=pltpu.SMEM)
    return pl.pallas_call(
        interact_kernel,
        out_shape=jax.ShapeDtypeStruct((samples, weight.shape[1]), BF16),
        in_specs=[vmem, vmem, vmem, vmem, smem, vmem, vmem],
        out_specs=vmem,
        scratch_shapes=[
            pltpu.VMEM((mixes * samples, width), BF16),
            pltpu.VMEM((features * mixes, samples), F32),
        ],
        compiler_params=pltpu.CompilerParams(vmem_limit_bytes=min(60 << 20, (8 << 20) + 3 * held)),
        name="interact",
    )(rows, sel, spread_c, mask, order, weight, bias)


def shards(
    n, tables, bag_rows, bag_lengths, row_counts, inverse, table_order, compress, top_weight, top_bias
):
    _, slots, most, pooling = bag_rows.shape
    tabs, vocab, width = tables.shape
    local = (jnp.arange(slots, dtype=jnp.int32) % tabs) * vocab
    active = jnp.arange(pooling, dtype=jnp.int32)[:, None] < bag_lengths[0].T[:, None, :]
    index = jnp.where(active, bag_rows[0].transpose(1, 2, 0) + local, tabs * vocab)
    rows, sel, spread_c, mask = exchange(
        n, most, index.reshape(most * pooling, slots), tables,
        inverse.T, table_order, row_counts[0], compress,
    )
    return interact(
        rows.reshape(slots * most, width), sel, spread_c, mask, table_order,
        top_weight, top_bias.reshape(1, -1),
    )


def solution(mesh):
    return jax.shard_map(
        functools.partial(shards, mesh.shape["dev"]),
        mesh=mesh,
        in_specs=(
            P("dev", None, None),
            P(("rep", "dev"), None, None, None),
            P(("rep", "dev"), None, None),
            P(("rep", "dev"), None),
            P(("rep", "dev"), None),
            P(),
            P(),
            P(),
            P(),
        ),
        out_specs=P(("rep", "dev"), None),
        check_vma=False,
    )
```

profile of v0, /device:TPU:0, one launch (start us, length us, event | category | flops | bytes accessed | tf_op | source)
XLA Modules:
  0.0 38.1 jit_solution(14524661708482330341)
XLA Ops:
  0.0 0.0 copy-start
  0.0 1.0 %bitcast_select_fusion = s32[32,4,64]{2,1,0:T(4,128)S(1)} fusion(s32[1,64,32,4]{1,3,2,0:T(4,128)} %param.10, s32[64]{0:T(128)S(1)} %fusion, s32[32,64]{1,0:T(8,128)} %bitcast.19), kind=kLoop, calls=%fused_computation | loop fusion | flops 24576 | bytes 73984 | tf_op jit(solution)/shard_map/jit(_where)/select_n | solution.py:306
  1.0 0.0 copy-start.1
  1.0 0.7 %copy-done.1 = s32[128,64]{0,1:T(8,128)S(1)} copy-done((s32[128,64]{0,1:T(8,128)S(1)}, s32[128,64]{0,1:T(8,128)}, u32[]{:S(2)}) %copy-start.1) | copy-done | bytes 32792
  1.7 0.0 copy-start.2
  1.7 0.7 %copy-done.2 = bf16[16,64]{1,0:T(8,128)(2,1)S(1)} copy-done((bf16[16,64]{1,0:T(8,128)(2,1)S(1)}, bf16[16,64]{1,0:T(8,128)(2,1)}, u32[]{:S(2)}) %copy-start.2) | copy-done | bytes 2072
  2.4 0.0 copy-start.4
  2.4 0.7 %copy-done.4 = s32[64]{0:T(128)S(1)} copy-done((s32[64]{0:T(128)S(1)}, s32[64]{0:T(128)}, u32[]{:S(2)}) %copy-start.4) | copy-done | bytes 280
  3.1 0.0 copy-start.5
  3.1 0.7 %copy-done.5 = s32[1,64]{1,0:T(1,128)S(1)} copy-done((s32[1,64]{1,0:T(1,128)S(1)}, s32[1,64]{1,0:T(1,128)}, u32[]{:S(2)}) %copy-start.5) | copy-done | bytes 280
  3.7 0.0 copy-start.3
  3.7 23.7 %exchange.1 = (bf16[16,128,128]{2,1,0:T(8,128)(2,1)S(1)}, bf16[128,2048]{1,0:T(8,128)(2,1)S(1)}, f32[16,2048]{1,0:T(8,128)S(1)}, f32[2048,128]{1,0:T(8,128)S(1)}) custom-call(s32[128,64]{1,0:T(8,128)S(1)} %bitcast.15, bf16[4,2048,128]{2,1,0:T(8,128)(2,1)} %tables_ref.1, s32[64,128]{1,0:T(8,128)S(1)} %bitcast.16, s32[64]{0:T(128)S(1)} %copy-done.4, ...), custom_call_target="tpu_custom_call" | custom-call | tf_op jit(solution)/shard_map/exchange/pallas_call | solution.py:179
  27.5 0.0 copy-done
  27.5 0.0 copy-done.3
  27.5 10.6 %interact.1 = bf16[128,512]{1,0:T(8,128)(2,1)} custom-call(bf16[2048,128]{1,0:T(8,128)(2,1)S(1)} %bitcast.14, bf16[128,2048]{1,0:T(8,128)(2,1)S(1)} %get-tuple-element.10.sel, f32[16,2048]{1,0:T(8,128)S(1)} %get-tuple-element.11.spread_c, f32[2048,128]{1,0:T(8,128)S(1)} %get-tuple-element.12.mask, s32[64]{0:T(128)S(1)} %copy-done.4, ...), custom_call_target="tpu_custom_call" | custom-call | tf_op jit(solution)/shard_map/interact/pallas_call | solution.py:285
  (1 shorter events, 0.0 us)
Async XLA Ops:
  0.0 27.5 %copy-start = (bf16[1024,512]{1,0:T(8,128)(2,1)S(1)}, bf16[1024,512]{1,0:T(8,128)(2,1)}, u32[]{:S(2)}) copy-start(bf16[1024,512]{1,0:T(8,128)(2,1)} %weight_ref.1) | copy-start | bytes 3145732
  1.0 0.8 %copy-start.1 = (s32[128,64]{0,1:T(8,128)S(1)}, s32[128,64]{0,1:T(8,128)}, u32[]{:S(2)}) copy-start(s32[128,64]{0,1:T(8,128)} %param.13) | copy-start | bytes 98308
  1.7 0.7 %copy-start.2 = (bf16[16,64]{1,0:T(8,128)(2,1)S(1)}, bf16[16,64]{1,0:T(8,128)(2,1)}, u32[]{:S(2)}) copy-start(bf16[16,64]{1,0:T(8,128)(2,1)} %compress_ref.1) | copy-start | bytes 6148
  2.4 0.7 %copy-start.4 = (s32[64]{0:T(128)S(1)}, s32[64]{0:T(128)}, u32[]{:S(2)}) copy-start(s32[64]{0:T(128)} %order_ref.3) | copy-start | bytes 772
  3.1 0.7 %copy-start.5 = (s32[1,64]{1,0:T(1,128)S(1)}, s32[1,64]{1,0:T(1,128)}, u32[]{:S(2)}) copy-start(s32[1,64]{1,0:T(1,128)} %param.12) | copy-start | bytes 772
  3.7 23.7 %copy-start.3 = (f32[512]{0:T(512)S(1)}, f32[512]{0:T(512)}, u32[]{:S(2)}) copy-start(f32[512]{0:T(512)} %param.17) | copy-start | bytes 6148
where the time goes:
time: 38.3 us; the launch traced here: 38.1 us
  Pallas kernels  34.3 us (90%)
  local copies, waits for them, and re-layouts  2.76 us (7%)
  other arithmetic  0.96 us (3%)
    pallas_call x1, Pallas kernels, exchange(): pl.pallas_call(functools.partial(exchange_kernel, n, most), out_shape=[ja...  23.7 us
    pallas_call x1, Pallas kernels, interact(): pl.pallas_call(interact_kernel, out_shape=jax.ShapeDtypeStruct((samples,...  10.6 us
    unnamed x12, local copies, waits for them, and re-layouts  2.76 us
    select_n x1, other arithmetic, shards(): jnp.where(active, bag_rows[0].transpose(1, 2, 0) + local, tabs * vocab)  0.95 us

commit v1 on v0

v1 whole, which is shorter than its diff:
```python
import functools

import jax
import jax.numpy as jnp
from jax import lax
from jax.experimental import pallas as pl
from jax.experimental.pallas import tpu as pltpu
from jax.sharding import PartitionSpec as P

F32 = jnp.float32
BF16 = jnp.bfloat16
I32 = jnp.int32
LANES = 128
PACK_GROUP, PACK_ROOM = 4, 80


def iota(shape, axis):
    return lax.broadcasted_iota(I32, shape, axis)


def flip(me, m, n):
    out, bit = me, 1
    while bit < n:
        out = out + ((m // bit) % 2) * (1 - 2 * ((me // bit) % 2)) * bit
        bit *= 2
    return out


def loop(start, stop, body, unroll=False):
    def step(i, carry):
        body(i)
        return carry

    lax.fori_loop(start, stop, step, 0, unroll=unroll)


def pack_ids(q, most, vocab, zero_row, counts, xt, lt, ids_out):
    pooling = ids_out.shape[1]
    tabs = PACK_GROUP
    shape = (2 * pooling, LANES)
    sub, lane = iota(shape, 0), iota(shape, 1)
    high, p = sub >= pooling, sub % pooling
    first, second = 2 * q * tabs, (2 * q + 1) * tabs
    off_a, off_b = jnp.int32(0), jnp.int32(0)
    ids = jnp.full(shape, zero_row, I32)
    for t in range(tabs):
        count_a, count_b = counts[first + t], counts[second + t]
        unit = lane - jnp.where(high, off_b, off_a)
        at = jnp.clip(unit, 0, most - 1)
        rows = jnp.where(high, xt[pl.ds(second + t, 1), :], xt[pl.ds(first + t, 1), :])
        lengths = jnp.where(high, lt[pl.ds(second + t, 1), :], lt[pl.ds(first + t, 1), :])
        row = jnp.take_along_axis(rows, at * pooling + p, axis=1, mode="promise_in_bounds")
        length = jnp.take_along_axis(lengths, at, axis=1, mode="promise_in_bounds")
        used = (unit >= 0) & (unit < jnp.where(high, count_b, count_a)) & (p < length)
        ids = jnp.where(used, row + t * vocab, ids)
        off_a, off_b = off_a + count_a, off_b + count_b
    ids_out[2 * q] = ids[:pooling]
    ids_out[2 * q + 1] = ids[pooling:]


def place_targets(g, order, counts, inv, targets, expand):
    tabs = PACK_GROUP
    feature = iota((1, expand.shape[1]), 1)
    off = jnp.int32(0)
    for t in range(tabs):
        s = g * tabs + t
        count = counts[s]
        row = inv[pl.ds(order[s], 1), :]
        row = jnp.where(row < count, row + off, -1)
        targets[g, t:t + 1, :] = row
        targets[g, tabs + t:tabs + t + 1, :] = pltpu.roll(row, row.shape[1] - 4, 1)
        off = off + count
        hot = jnp.where(feature == order[s], 1.0, 0.0)
        expand[pl.ds(g * 2 * tabs + t, 1), :] = hot
        expand[pl.ds(g * 2 * tabs + tabs + t, 1), :] = hot


def choose_rows(target, choice, at):
    samples = target.shape[1]
    lane = iota((16, LANES), 1)
    pairs = [blk * 8 + b for blk in range(samples // 8) for b in range(4)]
    for i in range(0, len(pairs), 2):
        wide = jnp.concatenate(
            [jnp.broadcast_to(target[:, c:c + 1], (8, LANES)) for c in pairs[i:i + 2]], axis=0
        )
        choice[at, i * 8:i * 8 + 16, :] = jnp.where(wide == lane, 1.0, 0.0).astype(BF16)


def exchange_kernel(
    n, most, room,
    bags_hbm, lens_hbm, tables_hbm, inv_hbm, order_hbm, counts_hbm, compress_hbm, weight_hbm,
    f_ref, mixer_ref, w_ref,
    bags, lens, tab16, inv, order, counts, compress, weight,
    tab32, xt, lt, ids_out, ids_in, pooled, staging, rows, targets, expand, choice,
    local, own_sem, id_send, id_recv, row_send, row_recv,
):
    me = lax.axis_index("dev")
    tabs, vocab, width = tab16.shape
    slots, samples = inv.shape
    mixes = compress.shape[0]
    pooling = ids_out.shape[1]
    zero_row = tabs * vocab
    small = n <= 16

    barrier = pltpu.get_barrier_semaphore()
    loop(1, n, lambda m: pl.semaphore_signal(barrier, inc=1, device_id={"dev": flip(me, m, n)}))

    copies = [
        pltpu.make_async_copy(src, dst, local.at[i])
        for i, (src, dst) in enumerate([
            (counts_hbm, counts), (bags_hbm, bags), (lens_hbm, lens), (order_hbm, order),
            (inv_hbm, inv), (compress_hbm, compress), (tables_hbm, tab16), (weight_hbm, weight),
        ])
    ]
    for copy in copies:
        copy.start()
    counts_in, bags_in, lens_in, order_in, inv_in, compress_in, tables_in, weight_in = copies

    bags_in.wait()
    xt[...] = bags[...].T
    lens_in.wait()
    lt[...] = jnp.concatenate(
        [lens[...], jnp.zeros((LANES - most, slots), I32)], axis=0
    ).T
    counts_in.wait()
    loop(
        0, n // 2, lambda q: pack_ids(q, most, vocab, zero_row, counts, xt, lt, ids_out),
        unroll=small,
    )
    pl.semaphore_wait(barrier, n - 1)

    def id_copy(m):
        peer = flip(me, m, n)
        return pltpu.make_async_remote_copy(
            src_ref=ids_out.at[peer], dst_ref=ids_in.at[m],
            send_sem=id_send.at[m], recv_sem=id_recv.at[m],
            device_id={"dev": peer},
        )

    def row_copy(m):
        peer = flip(me, m, n)
        return pltpu.make_async_remote_copy(
            src_ref=staging.at[m], dst_ref=rows.at[me],
            send_sem=row_send.at[m], recv_sem=row_recv.at[me],
            device_id={"dev": peer},
        )

    loop(1, n, lambda m: id_copy(m).start())
    own_ids = pltpu.make_async_copy(ids_out.at[me], ids_in.at[0], own_sem)
    own_ids.start()

    tables_in.wait()
    tab32[pl.ds(zero_row, 8), :] = jnp.zeros((8, width), F32)
    step = 256

    def widen(i):
        for t in range(tabs):
            base = pl.multiple_of(i * step, step)
            tab32[pl.ds(t * vocab + base, step), :] = tab16[t, pl.ds(base, step), :].astype(F32)

    loop(0, vocab // step, widen)

    order_in.wait()
    inv_in.wait()
    loop(0, n, lambda g: place_targets(g, order, counts, inv, targets, expand))
    if small:
        loop(0, n, lambda g: choose_rows(targets[g], choice, g))

    weight_in.wait()
    group = 8
    inner = group * mixes
    r, c = iota((inner, inner), 0), iota((inner, inner), 1)
    source = ((r // 8) % 2 * tabs + r % tabs) * mixes + 2 * (r // 16) + (r // 4) % 2
    reorder = jnp.where(c == source, 1.0, 0.0).astype(BF16)

    def order_weight(q):
        block = jnp.concatenate([weight[order[q * group + i]] for i in range(group)], axis=0)
        moved = jnp.dot(reorder, block, preferred_element_type=F32).astype(BF16)
        w_ref[:, pl.ds(pl.multiple_of(q * 16, 16), 16), :] = moved.reshape(mixes // 2, 16, -1)

    loop(0, slots // group, order_weight)

    compress_in.wait()
    across = f_ref.shape[1]
    spread = lax.dot_general(
        compress[...], expand[...].astype(BF16), (((1,), (1,)), ((), ())),
        preferred_element_type=F32,
    )
    sub, lane = iota((8, across), 0), iota((8, across), 1)
    same_half = (lane // tabs) % 2 == sub // 4
    for k in range(0, mixes, 2):
        for b in range(4):
            held = same_half & (sub % 4 == b)
            kept = [
                jnp.where(held, jnp.broadcast_to(spread[k + h:k + h + 1, :], (8, across)), 0.0)
                for h in range(2)
            ]
            mixer_ref[k * 8:k * 8 + 16, b * across:(b + 1) * across] = (
                jnp.concatenate(kept, axis=0).astype(BF16)
            )

    def pool(m, store):
        def row_block(i):
            at = pl.multiple_of(i * 16, 16)
            for r in range(16):
                total = None
                for p in range(pooling):
                    row = tab32[pl.ds(ids_in[m, p, at + r], 1), :]
                    total = row if total is None else total + row
                pooled[pl.ds(at + r, 1), :] = total

        loop(0, room // 16, row_block, unroll=True)
        store(pooled[...].astype(BF16))

    own_ids.wait()

    def store_own(value):
        rows[me] = value

    pool(0, store_own)

    def serve(m):
        id_copy(m).wait_recv()

        def store(value):
            staging[m] = value

        pool(m, store)
        row_copy(m).start()

    loop(1, n, serve)

    def select(i):
        q = flip(me // 2, i, n // 2)
        features = []
        for h in range(2):
            g = 2 * q + h
            at = g
            if not small:
                at = h
                choose_rows(targets[g], choice, h)
            packed = jnp.concatenate([rows[g], jnp.zeros((LANES - room, width), BF16)], axis=0)
            chosen = jnp.dot(choice[at], packed, preferred_element_type=F32)
            features.append(chosen.reshape(samples // 2, 8, width))
        f_ref[:, pl.ds(pl.multiple_of(q * 16, 16), 16), :] = (
            jnp.concatenate(features, axis=1).astype(BF16)
        )

    def arrival(m):
        peer = flip(me, m, n)
        pltpu.make_async_remote_copy(
            src_ref=staging.at[m], dst_ref=rows.at[peer],
            send_sem=row_send.at[m], recv_sem=row_recv.at[peer],
            device_id={"dev": peer},
        ).wait_recv()

    arrival(1)
    select(0)

    def collect(i):
        arrival(2 * i)
        arrival(2 * i + 1)
        select(i)

    loop(1, n // 2, collect)

    def finish(m):
        id_copy(m).wait_send()
        row_copy(m).wait_send()

    loop(1, n, finish)


def exchange(n, bags, lens, tables, inv, order, counts, compress, weight):
    tabs, vocab, width = tables.shape
    rows, slots = bags.shape
    most = lens.shape[0]
    pooling = rows // most
    samples, mixes, units = inv.shape[1], compress.shape[0], weight.shape[-1]
    room = PACK_ROOM
    assert tabs == PACK_GROUP and pooling == 4 and rows == LANES and n & (n - 1) == 0
    across = 2 * slots
    held = 3 * tables.size * 2 + 3 * weight.size * 2 + 3 * n * room * width * 4
    held += (samples * across * width + min(n, 16) * 4 * samples * LANES) * 2
    in_hbm = pl.BlockSpec(memory_space=pltpu.HBM)
    vmem = pl.BlockSpec(memory_space=pltpu.VMEM)
    operands = [
        pltpu.with_memory_space_constraint(x, pltpu.HBM)
        for x in (bags, lens, tables, inv, order, counts, compress, weight)
    ]
    return pl.pallas_call(
        functools.partial(exchange_kernel, n, most, room),
        out_shape=[
            jax.ShapeDtypeStruct((samples // 2, across, width), BF16),
            jax.ShapeDtypeStruct((mixes * 8, 4 * across), BF16),
            jax.ShapeDtypeStruct((mixes // 2, across, units), BF16),
        ],
        in_specs=[in_hbm] * 8,
        out_specs=[vmem] * 3,
        scratch_shapes=[
            pltpu.VMEM(bags.shape, I32),
            pltpu.VMEM(lens.shape, I32),
            pltpu.VMEM(tables.shape, BF16),
            pltpu.VMEM(inv.shape, I32),
            pltpu.SMEM(order.shape, I32),
            pltpu.SMEM(counts.shape, I32),
            pltpu.VMEM(compress.shape, BF16),
            pltpu.VMEM(weight.shape, BF16),
            pltpu.VMEM((tabs * vocab + 8, width), F32),
            pltpu.VMEM((slots, LANES), I32),
            pltpu.VMEM((slots, LANES), I32),
            pltpu.VMEM((n, pooling, LANES), I32),
            pltpu.SMEM((n, pooling, LANES), I32),
            pltpu.VMEM((room, width), F32),
            pltpu.VMEM((n, room, width), BF16),
            pltpu.VMEM((n, room, width), BF16),
            pltpu.VMEM((n, 2 * tabs, samples), I32),
            pltpu.VMEM((across, slots), F32),
            pltpu.VMEM((n if n <= 16 else 2, 4 * samples, LANES), BF16),
            pltpu.SemaphoreType.DMA((8,)),
            pltpu.SemaphoreType.DMA,
            pltpu.SemaphoreType.DMA((n,)),
            pltpu.SemaphoreType.DMA((n,)),
            pltpu.SemaphoreType.DMA((n,)),
            pltpu.SemaphoreType.DMA((n,)),
        ],
        compiler_params=pltpu.CompilerParams(
            collective_id=0, has_side_effects=True, vmem_limit_bytes=min(63 << 20, held + (6 << 20))
        ),
        name="exchange",
    )(*operands)


def interact_kernel(f_ref, mixer_ref, w_ref, bias_ref, out_ref, pairs):
    across, width = f_ref.shape[1:]
    mixes = mixer_ref.shape[0] // 8
    samples = out_ref.shape[0]
    sub, lane = iota((8, across), 0), iota((8, across), 1)
    first = sub < 4
    in_place = (lane // 4) % 2 == sub // 4
    mine = [sub % 4 == b for b in range(4)]

    def block(j):
        features = f_ref[pl.ds(j * 4, 4)].reshape(4 * across, width)
        mixed = jnp.dot(mixer_ref[...], features, preferred_element_type=F32).astype(BF16)
        products = lax.dot_general(
            mixed, features, (((1,), (1,)), ((), ())), preferred_element_type=F32
        )

        def of_mixture(k):
            parts = products[k * 8:k * 8 + 8, :]
            out = parts[:, :across]
            for b in range(1, 4):
                out = jnp.where(mine[b], parts[:, b * across:(b + 1) * across], out)
            return out

        for k in range(0, mixes, 2):
            even, odd = of_mixture(k), of_mixture(k + 1)
            stay, move = jnp.where(first, even, odd), jnp.where(first, odd, even)
            moved = jnp.where(first, pltpu.roll(move, 4, 1), pltpu.roll(move, across - 4, 1))
            pairs[pl.ds(pl.multiple_of(j * 8, 8), 8), k // 2 * across:(k // 2 + 1) * across] = (
                jnp.where(in_place, stay, moved)
            )

    loop(0, samples // 8, block)
    hidden = jnp.dot(
        pairs[...].astype(BF16), w_ref[...].reshape(mixes // 2 * across, -1),
        preferred_element_type=F32,
    ) + bias_ref[...]
    out_ref[...] = jnp.maximum(hidden, 0.0).astype(BF16)


def interact(features, mixer, weight, bias):
    pairs_of_samples, across, _ = features.shape
    samples, half_mixes, units = 2 * pairs_of_samples, weight.shape[0], weight.shape[2]
    held = (features.size + 2 * weight.size + mixer.size) * 2 + 6 * samples * half_mixes * across
    vmem = pl.BlockSpec(memory_space=pltpu.VMEM)
    return pl.pallas_call(
        interact_kernel,
        out_shape=jax.ShapeDtypeStruct((samples, units), BF16),
        in_specs=[vmem] * 4,
        out_specs=vmem,
        scratch_shapes=[pltpu.VMEM((samples, half_mixes * across), F32)],
        compiler_params=pltpu.CompilerParams(vmem_limit_bytes=min(63 << 20, held + (6 << 20))),
        name="interact",
    )(features, mixer, weight, bias)


def shards(
    n, tables, bag_rows, bag_lengths, row_counts, inverse, table_order, compress, top_weight, top_bias
):
    _, slots, most, pooling = bag_rows.shape
    mixes = compress.shape[0]
    features, mixer, weight = exchange(
        n, bag_rows[0].transpose(1, 2, 0).reshape(most * pooling, slots), bag_lengths[0].T, tables,
        inverse.T, table_order, row_counts[0], compress, top_weight.reshape(slots, mixes, -1),
    )
    return interact(features, mixer, weight, top_bias.reshape(1, -1))


def solution(mesh):
    return jax.shard_map(
        functools.partial(shards, mesh.shape["dev"]),
        mesh=mesh,
        in_specs=(
            P("dev", None, None),
            P(("rep", "dev"), None, None, None),
            P(("rep", "dev"), None, None),
            P(("rep", "dev"), None),
            P(("rep", "dev"), None),
            P(),
            P(),
            P(),
            P(),
        ),
        out_specs=P(("rep", "dev"), None),
        check_vma=False,
    )
```

time: 38.3 us -> 32.4 us (0.85)
  local copies, waits for them, and re-layouts: 2.76 us -> 0.01 us
  Pallas kernels: 34.3 us -> 32.2 us
  other arithmetic: 0.96 us -> 0 us
    pallas_call x1, Pallas kernels: 10.6 us -> 7.06 us  [interact(): pl.pallas_call(interact_kernel, out_shape=jax.ShapeDtypeStruct((samples,...]
    unnamed x12 -> x2, local copies, waits for them, and re-layouts: 2.76 us -> 0.01 us
    pallas_call x1, Pallas kernels: 23.7 us -> 25.2 us  [exchange(): pl.pallas_call(functools.partial(exchange_kernel, n, most, room), out_sha...]
    select_n x1 -> x0, other arithmetic: 0.95 us -> none  [shards(): jnp.where(active, bag_rows[0].transpose(1, 2, 0) + local, tabs * vocab)]
where the time goes in v1:
time: 32.4 us; the launch traced here: 32.2 us
  Pallas kernels  32.2 us (99%)
    pallas_call x1, Pallas kernels, exchange(): pl.pallas_call(functools.partial(exchange_kernel, n, most, room), out_sha...  25.2 us
    pallas_call x1, Pallas kernels, interact(): pl.pallas_call(interact_kernel, out_shape=jax.ShapeDtypeStruct((samples,...  7.06 us

profile of v1, /device:TPU:0, one launch (start us, length us, event | category | flops | bytes accessed | tf_op | source)
XLA Modules:
  0.0 32.2 jit_solution(3494430163006519330)
XLA Ops:
  0.0 0.0 copy-start
  0.0 25.2 %exchange.1 = (bf16[64,128,128]{2,1,0:T(8,128)(2,1)S(1)}, bf16[128,512]{1,0:T(8,128)(2,1)S(1)}, bf16[8,128,512]{2,1,0:T(8,128)(2,1)S(1)}) custom-call(s32[128,64]{1,0:T(8,128)} %bitcast.14, s32[32,64]{1,0:T(8,128)} %bitcast.16, bf16[4,2048,128]{2,1,0:T(8,128)(2,1)} %tables_hbm.1, s32[64,128]{1,0:T(8,128)} %bitcast.15, s32[64]{0:T(128)} %order_hbm.1, ...), custom_call_target="tpu_custom_call" | custom-call | tf_op jit(solution)/shard_map/exchange/pallas_call | solution.py:291
  25.2 0.0 copy-done
  25.2 7.1 %interact.1 = bf16[128,512]{1,0:T(8,128)(2,1)} custom-call(bf16[64,128,128]{2,1,0:T(8,128)(2,1)S(1)} %get-tuple-element.8.f_ref, bf16[128,512]{1,0:T(8,128)(2,1)S(1)} %get-tuple-element.9.mixer_ref, bf16[8,128,512]{2,1,0:T(8,128)(2,1)S(1)} %get-tuple-element.10.w_ref, f32[1,512]{1,0:T(1,128)S(1)} %bitcast.12), custom_call_target="tpu_custom_call" | custom-call | tf_op jit(solution)/shard_map/interact/pallas_call | solution.py:378
Async XLA Ops:
  0.0 25.2 %copy-start = (f32[512]{0:T(512)S(1)}, f32[512]{0:T(512)}, u32[]{:S(2)}) copy-start(f32[512]{0:T(512)} %param.17) | copy-start | bytes 6148

commit v2 on v1

--- a/solution.py
+++ b/solution.py
@@ -21,12 +21,20 @@
 def flip(me, m, n):
     out, bit = me, 1
     while bit < n:
-        out = out + ((m // bit) % 2) * (1 - 2 * ((me // bit) % 2)) * bit
+        if not isinstance(m, int):
+            out = out + ((m // bit) % 2) * (1 - 2 * ((me // bit) % 2)) * bit
+        elif m // bit % 2:
+            out = out + (bit - 2 * bit * ((me // bit) % 2))
         bit *= 2
     return out
 
 
 def loop(start, stop, body, unroll=False):
+    if unroll is True and stop - start <= 16:
+        for i in range(start, stop):
+            body(i)
+        return
+
     def step(i, carry):
         body(i)
         return carry
@@ -103,7 +111,11 @@
     small = n <= 16
 
     barrier = pltpu.get_barrier_semaphore()
-    loop(1, n, lambda m: pl.semaphore_signal(barrier, inc=1, device_id={"dev": flip(me, m, n)}))
+    loop(
+        1, n,
+        lambda m: pl.semaphore_signal(barrier, inc=1, device_id={"dev": flip(me, m, n)}),
+        unroll=small,
+    )
 
     copies = [
         pltpu.make_async_copy(src, dst, local.at[i])
@@ -127,6 +139,12 @@
         0, n // 2, lambda q: pack_ids(q, most, vocab, zero_row, counts, xt, lt, ids_out),
         unroll=small,
     )
+    order_in.wait()
+    inv_in.wait()
+    loop(0, n, lambda g: place_targets(g, order, counts, inv, targets, expand), unroll=4)
+    if small:
+        loop(0, n, lambda g: choose_rows(targets[g], choice, g), unroll=4)
+
     pl.semaphore_wait(barrier, n - 1)
 
     def id_copy(m):
@@ -145,7 +163,7 @@
             device_id={"dev": peer},
         )
 
-    loop(1, n, lambda m: id_copy(m).start())
+    loop(1, n, lambda m: id_copy(m).start(), unroll=small)
     own_ids = pltpu.make_async_copy(ids_out.at[me], ids_in.at[0], own_sem)
     own_ids.start()
 
@@ -159,12 +177,6 @@
             tab32[pl.ds(t * vocab + base, step), :] = tab16[t, pl.ds(base, step), :].astype(F32)
 
     loop(0, vocab // step, widen)
-
-    order_in.wait()
-    inv_in.wait()
-    loop(0, n, lambda g: place_targets(g, order, counts, inv, targets, expand))
-    if small:
-        loop(0, n, lambda g: choose_rows(targets[g], choice, g))
 
     weight_in.wait()
     group = 8
@@ -178,7 +190,7 @@
         moved = jnp.dot(reorder, block, preferred_element_type=F32).astype(BF16)
         w_ref[:, pl.ds(pl.multiple_of(q * 16, 16), 16), :] = moved.reshape(mixes // 2, 16, -1)
 
-    loop(0, slots // group, order_weight)
+    loop(0, slots // group, order_weight, unroll=4)
 
     compress_in.wait()
     across = f_ref.shape[1]
@@ -228,7 +240,7 @@
         pool(m, store)
         row_copy(m).start()
 
-    loop(1, n, serve)
+    lax.fori_loop(1, n, lambda i, c: (serve(i), c)[1], 0, unroll=small)
 
     def select(i):
         q = flip(me // 2, i, n // 2)
@@ -268,7 +280,7 @@
         id_copy(m).wait_send()
         row_copy(m).wait_send()
 
-    loop(1, n, finish)
+    loop(1, n, finish, unroll=small)
 
 
 def exchange(n, bags, lens, tables, inv, order, counts, compress, weight):
@@ -362,7 +374,7 @@
                 jnp.where(in_place, stay, moved)
             )
 
-    loop(0, samples // 8, block)
+    loop(0, samples // 8, block, unroll=samples <= LANES and across <= LANES)
     hidden = jnp.dot(
         pairs[...].astype(BF16), w_ref[...].reshape(mixes // 2 * across, -1),
         preferred_element_type=F32,

time: 32.4 us -> 25.6 us (0.79)
  Pallas kernels: 32.2 us -> 25.4 us
    pallas_call x1, Pallas kernels: 25.2 us -> 21.6 us  [exchange(): pl.pallas_call(functools.partial(exchange_kernel, n, most, room), out_sha...]
    pallas_call x1, Pallas kernels: 7.06 us -> 3.83 us  [interact(): pl.pallas_call(interact_kernel, out_shape=jax.ShapeDtypeStruct((samples,...]
where the time goes in v2:
time: 25.6 us; the launch traced here: 25.4 us
  Pallas kernels  25.4 us (99%)
    pallas_call x1, Pallas kernels, exchange(): pl.pallas_call(functools.partial(exchange_kernel, n, most, room), out_sha...  21.6 us
    pallas_call x1, Pallas kernels, interact(): pl.pallas_call(interact_kernel, out_shape=jax.ShapeDtypeStruct((samples,...  3.83 us

profile of v2, /device:TPU:0, one launch (start us, length us, event | category | flops | bytes accessed | tf_op | source)
XLA Modules:
  0.0 25.4 jit_solution(134325084368130896)
XLA Ops:
  0.0 0.0 copy-start
  0.0 21.6 %exchange.1 = (bf16[64,128,128]{2,1,0:T(8,128)(2,1)S(1)}, bf16[128,512]{1,0:T(8,128)(2,1)S(1)}, bf16[8,128,512]{2,1,0:T(8,128)(2,1)S(1)}) custom-call(s32[128,64]{1,0:T(8,128)} %bitcast.14, s32[32,64]{1,0:T(8,128)} %bitcast.16, bf16[4,2048,128]{2,1,0:T(8,128)(2,1)} %tables_hbm.1, s32[64,128]{1,0:T(8,128)} %bitcast.15, s32[64]{0:T(128)} %order_hbm.1, ...), custom_call_target="tpu_custom_call" | custom-call | tf_op jit(solution)/shard_map/exchange/pallas_call | solution.py:303
  21.6 0.0 copy-done
  21.6 3.8 %interact.1 = bf16[128,512]{1,0:T(8,128)(2,1)} custom-call(bf16[64,128,128]{2,1,0:T(8,128)(2,1)S(1)} %get-tuple-element.8.f_ref, bf16[128,512]{1,0:T(8,128)(2,1)S(1)} %get-tuple-element.9.mixer_ref, bf16[8,128,512]{2,1,0:T(8,128)(2,1)S(1)} %get-tuple-element.10.w_ref, f32[1,512]{1,0:T(1,128)S(1)} %bitcast.12), custom_call_target="tpu_custom_call" | custom-call | tf_op jit(solution)/shard_map/interact/pallas_call | solution.py:390
Async XLA Ops:
  0.0 21.6 %copy-start = (f32[512]{0:T(512)S(1)}, f32[512]{0:T(512)}, u32[]{:S(2)}) copy-start(f32[512]{0:T(512)} %param.17) | copy-start | bytes 6148

commit v3 on v2

--- a/solution.py
+++ b/solution.py
@@ -139,12 +139,6 @@
         0, n // 2, lambda q: pack_ids(q, most, vocab, zero_row, counts, xt, lt, ids_out),
         unroll=small,
     )
-    order_in.wait()
-    inv_in.wait()
-    loop(0, n, lambda g: place_targets(g, order, counts, inv, targets, expand), unroll=4)
-    if small:
-        loop(0, n, lambda g: choose_rows(targets[g], choice, g), unroll=4)
-
     pl.semaphore_wait(barrier, n - 1)
 
     def id_copy(m):
@@ -177,6 +171,10 @@
             tab32[pl.ds(t * vocab + base, step), :] = tab16[t, pl.ds(base, step), :].astype(F32)
 
     loop(0, vocab // step, widen)
+
+    order_in.wait()
+    inv_in.wait()
+    loop(0, n, lambda g: place_targets(g, order, counts, inv, targets, expand), unroll=4)
 
     weight_in.wait()
     group = 8
@@ -241,6 +239,8 @@
         row_copy(m).start()
 
     lax.fori_loop(1, n, lambda i, c: (serve(i), c)[1], 0, unroll=small)
+    if small:
+        loop(0, n, lambda g: choose_rows(targets[g], choice, g), unroll=4)
 
     def select(i):
         q = flip(me // 2, i, n // 2)

time: 25.6 us -> 23.8 us (0.930)
  Pallas kernels: 25.4 us -> 23.6 us
    pallas_call x1, Pallas kernels: 21.6 us -> 19.8 us  [exchange(): pl.pallas_call(functools.partial(exchange_kernel, n, most, room), out_sha...]
where the time goes in v3:
time: 23.8 us; the launch traced here: 23.6 us
  Pallas kernels  23.6 us (99%)
    pallas_call x1, Pallas kernels, exchange(): pl.pallas_call(functools.partial(exchange_kernel, n, most, room), out_sha...  19.8 us
    pallas_call x1, Pallas kernels, interact(): pl.pallas_call(interact_kernel, out_shape=jax.ShapeDtypeStruct((samples,...  3.82 us

profile of v3, /device:TPU:0, one launch (start us, length us, event | category | flops | bytes accessed | tf_op | source)
XLA Modules:
  0.0 23.6 jit_solution(16950410642297935292)
XLA Ops:
  0.0 0.0 copy-start
  0.0 19.8 %exchange.1 = (bf16[64,128,128]{2,1,0:T(8,128)(2,1)S(1)}, bf16[128,512]{1,0:T(8,128)(2,1)S(1)}, bf16[8,128,512]{2,1,0:T(8,128)(2,1)S(1)}) custom-call(s32[128,64]{1,0:T(8,128)} %bitcast.14, s32[32,64]{1,0:T(8,128)} %bitcast.16, bf16[4,2048,128]{2,1,0:T(8,128)(2,1)} %tables_hbm.1, s32[64,128]{1,0:T(8,128)} %bitcast.15, s32[64]{0:T(128)} %order_hbm.1, ...), custom_call_target="tpu_custom_call" | custom-call | tf_op jit(solution)/shard_map/exchange/pallas_call | solution.py:303
  19.8 0.0 copy-done
  19.8 3.8 %interact.1 = bf16[128,512]{1,0:T(8,128)(2,1)} custom-call(bf16[64,128,128]{2,1,0:T(8,128)(2,1)S(1)} %get-tuple-element.8.f_ref, bf16[128,512]{1,0:T(8,128)(2,1)S(1)} %get-tuple-element.9.mixer_ref, bf16[8,128,512]{2,1,0:T(8,128)(2,1)S(1)} %get-tuple-element.10.w_ref, f32[1,512]{1,0:T(1,128)S(1)} %bitcast.12), custom_call_target="tpu_custom_call" | custom-call | tf_op jit(solution)/shard_map/interact/pallas_call | solution.py:390
Async XLA Ops:
  0.0 19.8 %copy-start = (f32[512]{0:T(512)S(1)}, f32[512]{0:T(512)}, u32[]{:S(2)}) copy-start(f32[512]{0:T(512)} %param.17) | copy-start | bytes 6148

commit v4 on v3

--- a/solution.py
+++ b/solution.py
@@ -352,9 +352,7 @@
     in_place = (lane // 4) % 2 == sub // 4
     mine = [sub % 4 == b for b in range(4)]
 
-    def block(j):
-        features = f_ref[pl.ds(j * 4, 4)].reshape(4 * across, width)
-        mixed = jnp.dot(mixer_ref[...], features, preferred_element_type=F32).astype(BF16)
+    def block(j, features, mixed):
         products = lax.dot_general(
             mixed, features, (((1,), (1,)), ((), ())), preferred_element_type=F32
         )
@@ -374,7 +372,15 @@
                 jnp.where(in_place, stay, moved)
             )
 
-    loop(0, samples // 8, block, unroll=samples <= LANES and across <= LANES)
+    def two_blocks(i):
+        features = [f_ref[pl.ds(i * 8 + h * 4, 4)].reshape(4 * across, width) for h in range(2)]
+        mixed = jnp.dot(
+            mixer_ref[...], jnp.concatenate(features, axis=1), preferred_element_type=F32
+        ).astype(BF16)
+        for h in range(2):
+            block(2 * i + h, features[h], mixed[:, h * width:(h + 1) * width])
+
+    loop(0, samples // 16, two_blocks, unroll=samples <= LANES and across <= LANES)
     hidden = jnp.dot(
         pairs[...].astype(BF16), w_ref[...].reshape(mixes // 2 * across, -1),
         preferred_element_type=F32,

time: 23.8 us -> 22.8 us (0.958)
  Pallas kernels: 23.6 us -> 22.6 us
    pallas_call x1, Pallas kernels: 3.82 us -> 2.84 us  [interact(): pl.pallas_call(interact_kernel, out_shape=jax.ShapeDtypeStruct((samples,...]
where the time goes in v4:
time: 22.8 us; the launch traced here: 22.6 us
  Pallas kernels  22.6 us (99%)
    pallas_call x1, Pallas kernels, exchange(): pl.pallas_call(functools.partial(exchange_kernel, n, most, room), out_sha...  19.8 us
    pallas_call x1, Pallas kernels, interact(): pl.pallas_call(interact_kernel, out_shape=jax.ShapeDtypeStruct((samples,...  2.84 us

profile of v4, /device:TPU:0, one launch (start us, length us, event | category | flops | bytes accessed | tf_op | source)
XLA Modules:
  0.0 22.6 jit_solution(1305701179729108888)
XLA Ops:
  0.0 0.0 copy-start
  0.0 19.8 %exchange.1 = (bf16[64,128,128]{2,1,0:T(8,128)(2,1)S(1)}, bf16[128,512]{1,0:T(8,128)(2,1)S(1)}, bf16[8,128,512]{2,1,0:T(8,128)(2,1)S(1)}) custom-call(s32[128,64]{1,0:T(8,128)} %bitcast.14, s32[32,64]{1,0:T(8,128)} %bitcast.16, bf16[4,2048,128]{2,1,0:T(8,128)(2,1)} %tables_hbm.1, s32[64,128]{1,0:T(8,128)} %bitcast.15, s32[64]{0:T(128)} %order_hbm.1, ...), custom_call_target="tpu_custom_call" | custom-call | tf_op jit(solution)/shard_map/exchange/pallas_call | solution.py:303
  19.8 0.0 copy-done
  19.8 2.8 %interact.1 = bf16[128,512]{1,0:T(8,128)(2,1)} custom-call(bf16[64,128,128]{2,1,0:T(8,128)(2,1)S(1)} %get-tuple-element.8.f_ref, bf16[128,512]{1,0:T(8,128)(2,1)S(1)} %get-tuple-element.9.mixer_ref, bf16[8,128,512]{2,1,0:T(8,128)(2,1)S(1)} %get-tuple-element.10.w_ref, f32[1,512]{1,0:T(1,128)S(1)} %bitcast.12), custom_call_target="tpu_custom_call" | custom-call | tf_op jit(solution)/shard_map/interact/pallas_call | solution.py:396
Async XLA Ops:
  0.0 19.8 %copy-start = (f32[512]{0:T(512)S(1)}, f32[512]{0:T(512)}, u32[]{:S(2)}) copy-start(f32[512]{0:T(512)} %param.17) | copy-start | bytes 6148

commit v5 on v4

--- a/solution.py
+++ b/solution.py
@@ -27,6 +27,18 @@
             out = out + (bit - 2 * bit * ((me // bit) % 2))
         bit *= 2
     return out
+
+
+def turn(m, device, n, back=False):
+    def place(m):
+        return (m - 12 + n - 1) % (n - 1) + 1
+
+    hops = device % 2 + (device // 2) % 2 + device // 4
+    early, late = jnp.clip((5 * hops - 3) // 2, 1, n - 1), place(device)
+    at = m if back else place(m)
+    moved = jnp.where(at == late, early, jnp.where(at == early, late, at))
+    at = jnp.where(device == 0, at, moved)
+    return (at - 1 + 12 - 1) % (n - 1) + 1 if back else at
 
 
 def loop(start, stop, body, unroll=False):
@@ -113,7 +125,7 @@
     barrier = pltpu.get_barrier_semaphore()
     loop(
         1, n,
-        lambda m: pl.semaphore_signal(barrier, inc=1, device_id={"dev": flip(me, m, n)}),
+        lambda i: pl.semaphore_signal(barrier, inc=1, device_id={"dev": flip(me, n - i, n)}),
         unroll=small,
     )
 
@@ -144,20 +156,28 @@
     def id_copy(m):
         peer = flip(me, m, n)
         return pltpu.make_async_remote_copy(
+            src_ref=ids_out.at[peer], dst_ref=ids_in.at[turn(m, peer, n)],
+            send_sem=id_send.at[m], recv_sem=id_recv.at[turn(m, peer, n)],
+            device_id={"dev": peer},
+        )
+
+    def id_arrival(m):
+        peer = flip(me, turn(m, me, n, True), n)
+        return pltpu.make_async_remote_copy(
             src_ref=ids_out.at[peer], dst_ref=ids_in.at[m],
             send_sem=id_send.at[m], recv_sem=id_recv.at[m],
             device_id={"dev": peer},
         )
 
     def row_copy(m):
-        peer = flip(me, m, n)
+        peer = flip(me, turn(m, me, n, True), n)
         return pltpu.make_async_remote_copy(
             src_ref=staging.at[m], dst_ref=rows.at[me],
             send_sem=row_send.at[m], recv_sem=row_recv.at[me],
             device_id={"dev": peer},
         )
 
-    loop(1, n, lambda m: id_copy(m).start(), unroll=small)
+    loop(1, n, lambda i: id_copy(n - i).start(), unroll=small)
     own_ids = pltpu.make_async_copy(ids_out.at[me], ids_in.at[0], own_sem)
     own_ids.start()
 
@@ -222,15 +242,11 @@
         loop(0, room // 16, row_block, unroll=True)
         store(pooled[...].astype(BF16))
 
-    own_ids.wait()
-
     def store_own(value):
         rows[me] = value
 
-    pool(0, store_own)
-
     def serve(m):
-        id_copy(m).wait_recv()
+        id_arrival(m).wait_recv()
 
         def store(value):
             staging[m] = value
@@ -239,6 +255,8 @@
         row_copy(m).start()
 
     lax.fori_loop(1, n, lambda i, c: (serve(i), c)[1], 0, unroll=small)
+    own_ids.wait()
+    pool(0, store_own)
     if small:
         loop(0, n, lambda g: choose_rows(targets[g], choice, g), unroll=4)
 

time: 22.8 us -> 21.7 us (0.952)
  Pallas kernels: 22.6 us -> 21.6 us
    pallas_call x1, Pallas kernels: 19.8 us -> 18.7 us  [exchange(): pl.pallas_call(functools.partial(exchange_kernel, n, most, room), out_sha...]
where the time goes in v5:
time: 21.7 us; the launch traced here: 21.6 us
  Pallas kernels  21.6 us (100%)
    pallas_call x1, Pallas kernels, exchange(): pl.pallas_call(functools.partial(exchange_kernel, n, most, room), out_sha...  18.7 us
    pallas_call x1, Pallas kernels, interact(): pl.pallas_call(interact_kernel, out_shape=jax.ShapeDtypeStruct((samples,...  2.85 us

profile of v5, /device:TPU:0, one launch (start us, length us, event | category | flops | bytes accessed | tf_op | source)
XLA Modules:
  0.0 21.6 jit_solution(10888155192159960715)
XLA Ops:
  0.0 0.0 copy-start
  0.0 18.7 %exchange.1 = (bf16[64,128,128]{2,1,0:T(8,128)(2,1)S(1)}, bf16[128,512]{1,0:T(8,128)(2,1)S(1)}, bf16[8,128,512]{2,1,0:T(8,128)(2,1)S(1)}) custom-call(s32[128,64]{1,0:T(8,128)} %bitcast.14, s32[32,64]{1,0:T(8,128)} %bitcast.16, bf16[4,2048,128]{2,1,0:T(8,128)(2,1)} %tables_hbm.1, s32[64,128]{1,0:T(8,128)} %bitcast.15, s32[64]{0:T(128)} %order_hbm.1, ...), custom_call_target="tpu_custom_call" | custom-call | tf_op jit(solution)/shard_map/exchange/pallas_call | solution.py:321
  18.7 0.0 copy-done
  18.7 2.9 %interact.1 = bf16[128,512]{1,0:T(8,128)(2,1)} custom-call(bf16[64,128,128]{2,1,0:T(8,128)(2,1)S(1)} %get-tuple-element.8.f_ref, bf16[128,512]{1,0:T(8,128)(2,1)S(1)} %get-tuple-element.9.mixer_ref, bf16[8,128,512]{2,1,0:T(8,128)(2,1)S(1)} %get-tuple-element.10.w_ref, f32[1,512]{1,0:T(1,128)S(1)} %bitcast.12), custom_call_target="tpu_custom_call" | custom-call | tf_op jit(solution)/shard_map/interact/pallas_call | solution.py:414
Async XLA Ops:
  0.0 18.7 %copy-start = (f32[512]{0:T(512)S(1)}, f32[512]{0:T(512)}, u32[]{:S(2)}) copy-start(f32[512]{0:T(512)} %param.17) | copy-start | bytes 6148

commit v6 on v5

--- a/solution.py
+++ b/solution.py
@@ -361,7 +361,7 @@
     )(*operands)
 
 
-def interact_kernel(f_ref, mixer_ref, w_ref, bias_ref, out_ref, pairs):
+def interact_kernel(f_ref, mixer_ref, w_ref, bias_ref, out_ref, pairs, mixed):
     across, width = f_ref.shape[1:]
     mixes = mixer_ref.shape[0] // 8
     samples = out_ref.shape[0]
@@ -370,9 +370,10 @@
     in_place = (lane // 4) % 2 == sub // 4
     mine = [sub % 4 == b for b in range(4)]
 
-    def block(j, features, mixed):
+    def block(j):
+        features = f_ref[pl.ds(j * 4, 4)].reshape(4 * across, width)
         products = lax.dot_general(
-            mixed, features, (((1,), (1,)), ((), ())), preferred_element_type=F32
+            mixed[j], features, (((1,), (1,)), ((), ())), preferred_element_type=F32
         )
 
         def of_mixture(k):
@@ -390,15 +391,17 @@
                 jnp.where(in_place, stay, moved)
             )
 
-    def two_blocks(i):
+    def mix(i):
         features = [f_ref[pl.ds(i * 8 + h * 4, 4)].reshape(4 * across, width) for h in range(2)]
-        mixed = jnp.dot(
+        both = jnp.dot(
             mixer_ref[...], jnp.concatenate(features, axis=1), preferred_element_type=F32
         ).astype(BF16)
         for h in range(2):
-            block(2 * i + h, features[h], mixed[:, h * width:(h + 1) * width])
-
-    loop(0, samples // 16, two_blocks, unroll=samples <= LANES and across <= LANES)
+            mixed[2 * i + h] = both[:, h * width:(h + 1) * width]
+
+    flat = samples <= LANES and across <= LANES
+    loop(0, samples // 16, mix, unroll=flat)
+    loop(0, samples // 8, block, unroll=flat)
     hidden = jnp.dot(
         pairs[...].astype(BF16), w_ref[...].reshape(mixes // 2 * across, -1),
         preferred_element_type=F32,
@@ -416,7 +419,10 @@
         out_shape=jax.ShapeDtypeStruct((samples, units), BF16),
         in_specs=[vmem] * 4,
         out_specs=vmem,
-        scratch_shapes=[pltpu.VMEM((samples, half_mixes * across), F32)],
+        scratch_shapes=[
+            pltpu.VMEM((samples, half_mixes * across), F32),
+            pltpu.VMEM((samples // 8, mixer.shape[0], features.shape[2]), BF16),
+        ],
         compiler_params=pltpu.CompilerParams(vmem_limit_bytes=min(63 << 20, held + (6 << 20))),
         name="interact",
     )(features, mixer, weight, bias)

time: 21.7 us -> 20.9 us (0.963)
  Pallas kernels: 21.6 us -> 20.7 us
    pallas_call x1, Pallas kernels: 2.85 us -> 1.97 us  [interact(): pl.pallas_call(interact_kernel, out_shape=jax.ShapeDtypeStruct((samples,...]
where the time goes in v6:
time: 20.9 us; the launch traced here: 20.7 us
  Pallas kernels  20.7 us (99%)
    pallas_call x1, Pallas kernels, exchange(): pl.pallas_call(functools.partial(exchange_kernel, n, most, room), out_sha...  18.7 us
    pallas_call x1, Pallas kernels, interact(): pl.pallas_call(interact_kernel, out_shape=jax.ShapeDtypeStruct((samples,...  1.97 us

profile of v6, /device:TPU:0, one launch (start us, length us, event | category | flops | bytes accessed | tf_op | source)
XLA Modules:
  0.0 20.7 jit_solution(11240761362873855270)
XLA Ops:
  0.0 0.0 copy-start
  0.0 18.7 %exchange.1 = (bf16[64,128,128]{2,1,0:T(8,128)(2,1)S(1)}, bf16[128,512]{1,0:T(8,128)(2,1)S(1)}, bf16[8,128,512]{2,1,0:T(8,128)(2,1)S(1)}) custom-call(s32[128,64]{1,0:T(8,128)} %bitcast.14, s32[32,64]{1,0:T(8,128)} %bitcast.16, bf16[4,2048,128]{2,1,0:T(8,128)(2,1)} %tables_hbm.1, s32[64,128]{1,0:T(8,128)} %bitcast.15, s32[64]{0:T(128)} %order_hbm.1, ...), custom_call_target="tpu_custom_call" | custom-call | tf_op jit(solution)/shard_map/exchange/pallas_call | solution.py:321
  18.7 0.0 copy-done
  18.7 2.0 %interact.1 = bf16[128,512]{1,0:T(8,128)(2,1)} custom-call(bf16[64,128,128]{2,1,0:T(8,128)(2,1)S(1)} %get-tuple-element.8.f_ref, bf16[128,512]{1,0:T(8,128)(2,1)S(1)} %get-tuple-element.9.mixer_ref, bf16[8,128,512]{2,1,0:T(8,128)(2,1)S(1)} %get-tuple-element.10.w_ref, f32[1,512]{1,0:T(1,128)S(1)} %bitcast.12), custom_call_target="tpu_custom_call" | custom-call | tf_op jit(solution)/shard_map/interact/pallas_call | solution.py:417
Async XLA Ops:
  0.0 18.7 %copy-start = (f32[512]{0:T(512)S(1)}, f32[512]{0:T(512)}, u32[]{:S(2)}) copy-start(f32[512]{0:T(512)} %param.17) | copy-start | bytes 6148

commit v7 on v6

--- a/solution.py
+++ b/solution.py
@@ -19,26 +19,26 @@
 
 
 def flip(me, m, n):
-    out, bit = me, 1
-    while bit < n:
-        if not isinstance(m, int):
-            out = out + ((m // bit) % 2) * (1 - 2 * ((me // bit) % 2)) * bit
-        elif m // bit % 2:
-            out = out + (bit - 2 * bit * ((me // bit) % 2))
-        bit *= 2
-    return out
+    return me ^ m
+
+
+def low(m, bit):
+    return (m >> (bit.bit_length() - 1)) & 1
+
+
+def wrap(m, n):
+    return jnp.where(m >= n, m - (n - 1), m)
 
 
 def turn(m, device, n, back=False):
-    def place(m):
-        return (m - 12 + n - 1) % (n - 1) + 1
-
-    hops = device % 2 + (device // 2) % 2 + device // 4
-    early, late = jnp.clip((5 * hops - 3) // 2, 1, n - 1), place(device)
-    at = m if back else place(m)
+    first = n - n // 4
+    hops = low(device, 1) + low(device, 2) + (device >> 2)
+    early = jnp.clip(2 * hops, 1, n - 1)
+    late = wrap(device + n - first, n)
+    at = m if back else wrap(m + n - first, n)
     moved = jnp.where(at == late, early, jnp.where(at == early, late, at))
     at = jnp.where(device == 0, at, moved)
-    return (at - 1 + 12 - 1) % (n - 1) + 1 if back else at
+    return wrap(at + first - 1, n) if back else at
 
 
 def loop(start, stop, body, unroll=False):
@@ -292,7 +292,7 @@
         arrival(2 * i + 1)
         select(i)
 
-    loop(1, n // 2, collect)
+    loop(1, n // 2, collect, unroll=small)
 
     def finish(m):
         id_copy(m).wait_send()

time: 20.9 us -> 20.7 us (level)
  no operation moved by 1% of the time
where the time goes in v7:
time: 20.7 us; the launch traced here: 20.5 us
  Pallas kernels  20.5 us (99%)
    pallas_call x1, Pallas kernels, exchange(): pl.pallas_call(functools.partial(exchange_kernel, n, most, room), out_sha...  18.6 us
    pallas_call x1, Pallas kernels, interact(): pl.pallas_call(interact_kernel, out_shape=jax.ShapeDtypeStruct((samples,...  1.97 us

profile of v7, /device:TPU:0, one launch (start us, length us, event | category | flops | bytes accessed | tf_op | source)
XLA Modules:
  0.0 20.5 jit_solution(11399916998815610039)
XLA Ops:
  0.0 0.0 copy-start
  0.0 18.6 %exchange.1 = (bf16[64,128,128]{2,1,0:T(8,128)(2,1)S(1)}, bf16[128,512]{1,0:T(8,128)(2,1)S(1)}, bf16[8,128,512]{2,1,0:T(8,128)(2,1)S(1)}) custom-call(s32[128,64]{1,0:T(8,128)} %bitcast.14, s32[32,64]{1,0:T(8,128)} %bitcast.16, bf16[4,2048,128]{2,1,0:T(8,128)(2,1)} %tables_hbm.1, s32[64,128]{1,0:T(8,128)} %bitcast.15, s32[64]{0:T(128)} %order_hbm.1, ...), custom_call_target="tpu_custom_call" | custom-call | tf_op jit(solution)/shard_map/exchange/pallas_call | solution.py:321
  18.6 0.0 copy-done
  18.6 2.0 %interact.1 = bf16[128,512]{1,0:T(8,128)(2,1)} custom-call(bf16[64,128,128]{2,1,0:T(8,128)(2,1)S(1)} %get-tuple-element.8.f_ref, bf16[128,512]{1,0:T(8,128)(2,1)S(1)} %get-tuple-element.9.mixer_ref, bf16[8,128,512]{2,1,0:T(8,128)(2,1)S(1)} %get-tuple-element.10.w_ref, f32[1,512]{1,0:T(1,128)S(1)} %bitcast.12), custom_call_target="tpu_custom_call" | custom-call | tf_op jit(solution)/shard_map/interact/pallas_call | solution.py:417
Async XLA Ops:
  0.0 18.6 %copy-start = (f32[512]{0:T(512)S(1)}, f32[512]{0:T(512)}, u32[]{:S(2)}) copy-start(f32[512]{0:T(512)} %param.17) | copy-start | bytes 6148

commit v8 on v7

--- a/solution.py
+++ b/solution.py
@@ -284,6 +284,7 @@
             device_id={"dev": peer},
         ).wait_recv()
 
+    loop(1, n, lambda m: id_copy(m).wait_send(), unroll=small)
     arrival(1)
     select(0)
 
@@ -292,13 +293,9 @@
         arrival(2 * i + 1)
         select(i)
 
-    loop(1, n // 2, collect, unroll=small)
-
-    def finish(m):
-        id_copy(m).wait_send()
-        row_copy(m).wait_send()
-
-    loop(1, n, finish, unroll=small)
+    loop(1, n // 2 - 1, collect, unroll=small)
+    loop(1, n, lambda m: row_copy(m).wait_send(), unroll=small)
+    collect(n // 2 - 1)
 
 
 def exchange(n, bags, lens, tables, inv, order, counts, compress, weight):

time: 20.7 us -> 20.6 us (level)
  no operation moved by 1% of the time
where the time goes in v8:
time: 20.6 us; the launch traced here: 20.4 us
  Pallas kernels  20.4 us (99%)
    pallas_call x1, Pallas kernels, exchange(): pl.pallas_call(functools.partial(exchange_kernel, n, most, room), out_sha...  18.4 us
    pallas_call x1, Pallas kernels, interact(): pl.pallas_call(interact_kernel, out_shape=jax.ShapeDtypeStruct((samples,...  1.97 us

profile of v8, /device:TPU:0, one launch (start us, length us, event | category | flops | bytes accessed | tf_op | source)
XLA Modules:
  0.0 20.4 jit_solution(15861407583479356699)
XLA Ops:
  0.0 0.0 copy-start
  0.0 18.4 %exchange.1 = (bf16[64,128,128]{2,1,0:T(8,128)(2,1)S(1)}, bf16[128,512]{1,0:T(8,128)(2,1)S(1)}, bf16[8,128,512]{2,1,0:T(8,128)(2,1)S(1)}) custom-call(s32[128,64]{1,0:T(8,128)} %bitcast.14, s32[32,64]{1,0:T(8,128)} %bitcast.16, bf16[4,2048,128]{2,1,0:T(8,128)(2,1)} %tables_hbm.1, s32[64,128]{1,0:T(8,128)} %bitcast.15, s32[64]{0:T(128)} %order_hbm.1, ...), custom_call_target="tpu_custom_call" | custom-call | tf_op jit(solution)/shard_map/exchange/pallas_call | solution.py:318
  18.4 0.0 copy-done
  18.4 2.0 %interact.1 = bf16[128,512]{1,0:T(8,128)(2,1)} custom-call(bf16[64,128,128]{2,1,0:T(8,128)(2,1)S(1)} %get-tuple-element.8.f_ref, bf16[128,512]{1,0:T(8,128)(2,1)S(1)} %get-tuple-element.9.mixer_ref, bf16[8,128,512]{2,1,0:T(8,128)(2,1)S(1)} %get-tuple-element.10.w_ref, f32[1,512]{1,0:T(1,128)S(1)} %bitcast.12), custom_call_target="tpu_custom_call" | custom-call | tf_op jit(solution)/shard_map/interact/pallas_call | solution.py:414
Async XLA Ops:
  0.0 18.4 %copy-start = (f32[512]{0:T(512)S(1)}, f32[512]{0:T(512)}, u32[]{:S(2)}) copy-start(f32[512]{0:T(512)} %param.17) | copy-start | bytes 6148
